TPU v7x, 128 devices: a whole 4x4x4 slice. The times are simulated.
128 devices in a mesh: ga: 16 (over x, z_hi, core), ba: 8 (over y, z_lo).
Axes of the slice: x: 4, y: 4, z: 4 (z_hi: 2, z_lo: 2; z = z_hi * 2 + z_lo), core: 2. Of those that a mesh axis runs over, the one named last changes fastest.
Arguments:
- psi: float32 [2, 32768, 2048], P(None, 'ga', 'ba'), may hold values from -0.15625 to 0.15625
- dpsi: float32 [2, 32768, 512], P(None, 'ga', 'ba'), may hold values from -6 to 6
- band_weight: float32 [2048], replicated, may hold values from 0.25 to 1
- panel_band: int32 [16], P('ba'), may hold values from 0 to 15, each once
- slab_offset: int32 [16], replicated, may hold values from 0 to 2047
Outputs:
- projected: float32 [2, 32768, 512], P(None, 'ga', 'ba')
Inputs may be any that keep to these rules, and one draw needn't show every extreme that they name: panel_band is a permutation of the panel numbers.
All inputs are finite; a program needn't handle non-finite values.
Results may differ from a plain program's by a relative error of at most 0.00012.
Values sent between devices are 32-bit elements; how exact they have to be, the bound alone decides.
A program may use at most 128 MiB of HBM per device.

v0:
```python
import jax
import jax.numpy as jnp
from jax import lax
from jax.sharding import PartitionSpec as P

PANEL = 128


def split_up(value, dim, count):
    before, after = (value.shape[:dim], value.shape[dim + 1 :])
    return jnp.moveaxis(value.reshape(*before, count, -1, *after), dim, 0)


def edges_of(length, count):
    turn = length // count
    if turn >= 8:
        turn -= turn % 8
    return [turn * k for k in range(1, count)]


def in_order(blocks, dim):
    lengths = list(blocks.shape[1:])
    lengths[dim] *= blocks.shape[0]
    return jnp.moveaxis(blocks, 0, dim).reshape(lengths)


def cut_exchange(value, axis, pieces, split_dim, concat_dim):
    blocks = split_up(value, split_dim, lax.axis_size(axis))
    split_at = max(range(1, max(2, blocks.ndim - 1)), key=lambda d: blocks.shape[d])
    done = []
    for slab in jnp.split(blocks, edges_of(blocks.shape[split_at], pieces), axis=split_at):
        if slab.size:
            done.append(lax.all_to_all(slab, axis, split_axis=0, concat_axis=0, tiled=True))
    return in_order(jnp.concatenate(done, axis=split_at), concat_dim)


def from_everyone(value, axis):
    count = lax.axis_size(axis)
    return lax.all_to_all(
        jnp.broadcast_to(value[None], (count, *value.shape)), axis, 0, 0, tiled=True
    )


def gather_directly(value, axis, dim):
    blocks = from_everyone(value, axis)
    return in_order(blocks, dim)


def tdot(left, right):
    return lax.dot_general(
        left,
        right,
        (((0,), (0,)), ((), ())),
        precision=lax.Precision.HIGHEST,
        preferred_element_type=jnp.float32,
    )


def mdot(left, right):
    return jnp.dot(left, right, precision=lax.Precision.HIGHEST, preferred_element_type=jnp.float32)


def margin_of(waves, columns):
    over_re = tdot(waves[0], columns[0]) + tdot(waves[1], columns[1])
    over_im = tdot(waves[0], columns[1]) - tdot(waves[1], columns[0])
    return jnp.stack([over_re, over_im])


def correct_with(waves, weighted):
    corr_re = mdot(waves[0], weighted[0]) - mdot(waves[1], weighted[1])
    corr_im = mdot(waves[0], weighted[1]) + mdot(waves[1], weighted[0])
    return jnp.stack([corr_re, corr_im])


def weights_for(band_weight, panels):
    table = band_weight.reshape(-1, PANEL)
    onehot = (panels[:, None] == jnp.arange(table.shape[0], dtype=jnp.int32)[None, :]).astype(
        jnp.float32
    )
    return mdot(onehot, table).reshape(-1)


def per_device(psi, dpsi, band_weight, panel_band, slab_offset):
    offset = slab_offset[lax.axis_index("ga")]
    aligned = jnp.roll(dpsi, -offset, axis=1)
    row_waves, row_columns = (
        cut_exchange(psi, "ba", 2, 1, 2),
        cut_exchange(aligned, "ba", 2, 1, 2),
    )
    all_panels = gather_directly(panel_band, "ba", 0)
    full_weight = weights_for(band_weight, all_panels)
    margin = lax.psum(margin_of(row_waves, row_columns), ("ga", "ba"))
    weighted = margin * full_weight[None, :, None]
    row_result = row_columns - correct_with(row_waves, weighted)
    result = lax.all_to_all(row_result, "ba", split_axis=2, concat_axis=1, tiled=True)
    return jnp.roll(result, offset, axis=1)


def solution(mesh):
    in_specs = (P(None, "ga", "ba"), P(None, "ga", "ba"), P(), P("ba"), P())
    out_specs = P(None, "ga", "ba")
    return jax.shard_map(
        per_device, mesh=mesh, in_specs=in_specs, out_specs=out_specs, check_vma=False
    )
```

profile of v0, /device:TPU:2, one launch (start us, length us, event | category | flops | bytes accessed | tf_op | source)
XLA Modules:
  0.0 354.8 jit_solution(3534208202760883374)
XLA Ops:
  6.5 1.2 dynamic_slice.6
  8.9 1.8 fusion.9
  10.8 0.3 copy.34
  11.1 0.1 fusion.15
  11.2 0.9 copy.21
  12.1 5.8 %all-to-all-start.1 = ((f32[8,2,128,64]{2,3,1,0:T(8,128)}), f32[8,2,128,64]{2,3,1,0:T(8,128)S(1)}, u32[]{:S(2)}, u32[]{:S(2)}) async-start(f32[8,2,128,64]{2,3,1,0:T(8,128)} %copy.21), calls=%async_computation.1 | async-start | bytes 1048576 | tf_op jit(solution)/shard_map/all_to_all | solution.py:33
  17.9 0.9 copy.20
  18.8 8.7 %all-to-all-done.1 = f32[8,2,128,64]{2,3,1,0:T(8,128)S(1)} async-done(((f32[8,2,128,64]{2,3,1,0:T(8,128)}), f32[8,2,128,64]{2,3,1,0:T(8,128)S(1)}, u32[]{:S(2)}, u32[]{:S(2)}) %all-to-all-start.1) | async-done | bytes 524320 | tf_op jit(solution)/shard_map/all_to_all | solution.py:33
  27.5 3.5 all-to-all-start
  31.0 4.0 %fusion.13 = (f32[8,2,128,256]{3,2,0,1:T(8,128)}, f32[8,2,128,256]{3,2,0,1:T(8,128)S(1)}) fusion(f32[8,2,256,256]{3,2,0,1:T(8,128)} %bitcast.83), kind=kLoop, calls=%fused_computation.29 | loop fusion | bytes 8388608 | tf_op jit(solution)/shard_map/split | solution.py:31
  34.9 1.6 copy.25
  36.5 3.4 all-to-all-done
  39.9 3.6 %all-to-all-start.3 = ((f32[8,2,128,256]{3,2,1,0:T(8,128)}), f32[8,2,128,256]{3,2,1,0:T(8,128)S(1)}, u32[]{:S(2)}, u32[]{:S(2)}) async-start(f32[8,2,128,256]{3,2,1,0:T(8,128)} %copy.25), calls=%async_computation.3 | async-start | bytes 4194304 | tf_op jit(solution)/shard_map/all_to_all | solution.py:33
  43.5 3.1 copy.24
  46.6 26.9 %all-to-all-done.3 = f32[8,2,128,256]{3,2,1,0:T(8,128)S(1)} async-done(((f32[8,2,128,256]{3,2,1,0:T(8,128)}), f32[8,2,128,256]{3,2,1,0:T(8,128)S(1)}, u32[]{:S(2)}, u32[]{:S(2)}) %all-to-all-start.3) | async-done | bytes 2097184 | tf_op jit(solution)/shard_map/all_to_all | solution.py:33
  73.5 4.3 %all-to-all-start.2 = ((f32[8,2,128,256]{3,2,1,0:T(8,128)}), f32[8,2,128,256]{3,2,1,0:T(8,128)}, u32[]{:S(2)}, u32[]{:S(2)}) async-start(f32[8,2,128,256]{3,2,1,0:T(8,128)} %copy.24), calls=%async_computation.2 | async-start | bytes 4194304 | tf_op jit(solution)/shard_map/all_to_all | solution.py:33
  77.9 1.1 copy_bitcast_fusion
  79.0 0.1 fusion.14
  79.1 1.9 copy.27
  81.0 26.4 %all-to-all-done.2 = f32[8,2,128,256]{3,2,1,0:T(8,128)} async-done(((f32[8,2,128,256]{3,2,1,0:T(8,128)}), f32[8,2,128,256]{3,2,1,0:T(8,128)}, u32[]{:S(2)}, u32[]{:S(2)}) %all-to-all-start.2) | async-done | bytes 2097184 | tf_op jit(solution)/shard_map/all_to_all | solution.py:33
  107.4 3.3 copy.26
  110.7 2.1 maximum_bitcast_fusion
  112.8 0.4 fusion.12
  113.2 3.7 %fusion.17 = f32[2048,512]{1,0:T(8,128)S(1)} fusion(f32[256,2048]{0,1:T(8,128)S(1)} %bitcast.68, f32[256,512]{0,1:T(8,128)S(1)} %bitcast.76), kind=kOutput, calls=%fused_computation.33 | convolution fusion | flops 3221225472 | bytes 6815744 | tf_op jit(solution)/shard_map/dot_general | solution.py:50
  116.9 3.7 %fusion.16 = f32[2048,512]{1,0:T(8,128)S(1)} fusion(f32[256,2048]{0,1:T(8,128)S(1)} %bitcast.69, f32[256,512]{0,1:T(8,128)S(1)} %bitcast.78), kind=kOutput, calls=%fused_computation.32 | convolution fusion | flops 3221225472 | bytes 6815744 | tf_op jit(solution)/shard_map/dot_general | solution.py:50
  120.7 3.8 %subtract_bitcast_fusion = f32[1,2048,512]{2,1,0:T(8,128)S(1)} fusion(f32[2048,512]{1,0:T(8,128)S(1)} %fusion.17, f32[256,2048]{0,1:T(8,128)S(1)} %bitcast.72, f32[256,512]{0,1:T(8,128)S(1)} %bitcast.79), kind=kOutput, calls=%fused_computation.5 | convolution fusion | flops 3222274048 | bytes 11010048 | tf_op jit(solution)/shard_map/dot_general | solution.py:50
  124.4 15.3 %add_bitcast_fusion = f32[1,2048,512]{2,1,0:T(8,128)S(1)} fusion(f32[2048,512]{1,0:T(8,128)S(1)} %fusion.16, f32[256,2048]{0,1:T(8,128)S(1)} %bitcast.73, f32[256,512]{0,1:T(8,128)S(1)} %bitcast.77), kind=kOutput, calls=%fused_computation.6 | convolution fusion | flops 3222274048 | bytes 11010048 | tf_op jit(solution)/shard_map/dot_general | solution.py:50
  139.7 4.2 %pad_maximum_fusion = f32[2,2048,512]{2,1,0:T(8,128)} fusion(f32[1,2048,512]{2,1,0:T(8,128)S(1)} %subtract_bitcast_fusion, f32[1,2048,512]{2,1,0:T(8,128)S(1)} %add_bitcast_fusion), kind=kLoop, calls=%fused_computation | loop fusion | flops 2097152 | bytes 16777216 | tf_op jit(solution)/shard_map/stack | solution.py:66
  144.0 0.6 copy-done.6
  144.6 8.5 %all_to_all.44 = s32[8,1,2]{2,1,0:T(1,128)S(1)} all-to-all(s32[8,1,2]{2,1,0:T(1,128)S(1)} %broadcast_in_dim.2), channel_id=1, replica_groups=mesh['ga'=16,'ba'=8] {'ba'}, dimensions={0} | all-to-all | bytes 128 | tf_op jit(solution)/shard_map/all_to_all | solution.py:39
  153.1 0.6 broadcast.7
  153.7 0.7 reduce.3
  154.4 0.1 eq.17
  154.5 0.2 convolution_bitcast_fusion
  154.7 1.3 copy.28
  156.0 148.4 %all-reduce.2.cloned.1.call-done = f32[2,2048,512]{2,1,0:T(8,128)} async-done(((f32[2,2048,512]{2,1,0:T(8,128)}), f32[2,2048,512]{2,1,0:T(8,128)}) %all-reduce.2.cloned.1.call-update) | async-done | bytes 8388624 | tf_op jit(solution)/shard_map/psum | solution.py:92
  304.4 4.1 %broadcast_multiply_fusion = f32[2,2048,512]{2,1,0:T(8,128)S(1)} fusion(f32[2,2048,512]{2,1,0:T(8,128)} %all-reduce.2.cloned.1.call-done, f32[2048]{0:T(1024)S(1)} %convolution_bitcast_fusion), kind=kLoop, calls=%fused_computation.4 | loop fusion | flops 2097152 | bytes 16785408 | tf_op jit(solution)/shard_map/mul | solution.py:93
  308.6 3.8 %fusion = f32[256,512]{1,0:T(8,128)S(1)} fusion(f32[256,2048]{0,1:T(8,128)S(1)} %bitcast.74, f32[2,2048,512]{2,1,0:T(8,128)S(1)} %broadcast_multiply_fusion), kind=kOutput, calls=%fused_computation.7 | convolution fusion | flops 3221225472 | bytes 6815744 | tf_op jit(solution)/shard_map/dot_general | solution.py:60
  312.4 3.9 %fusion.1 = f32[256,512]{1,0:T(8,128)S(1)} fusion(f32[256,2048]{0,1:T(8,128)S(1)} %bitcast.70, f32[2,2048,512]{2,1,0:T(8,128)S(1)} %broadcast_multiply_fusion), kind=kOutput, calls=%fused_computation.8 | convolution fusion | flops 3221225472 | bytes 6815744 | tf_op jit(solution)/shard_map/dot_general | solution.py:60
  316.3 4.1 %fusion.7 = f32[1,256,512]{2,1,0:T(8,128)S(1)} fusion(f32[256,512]{1,0:T(8,128)S(1)} %fusion, f32[256,2048]{0,1:T(8,128)S(1)} %bitcast.71, f32[2,2048,512]{2,1,0:T(8,128)S(1)} %broadcast_multiply_fusion), kind=kOutput, calls=%fused_computation.18 | convolution fusion | flops 3221356544 | bytes 7340032 | tf_op jit(solution)/shard_map/dot_general | solution.py:60
  320.4 3.8 %fusion.5 = f32[1,256,512]{2,1,0:T(8,128)S(1)} fusion(f32[256,512]{1,0:T(8,128)S(1)} %fusion.1, f32[256,2048]{0,1:T(8,128)S(1)} %bitcast.75, f32[2,2048,512]{2,1,0:T(8,128)S(1)} %broadcast_multiply_fusion), kind=kOutput, calls=%fused_computation.16 | convolution fusion | flops 3221356544 | bytes 7340032 | tf_op jit(solution)/shard_map/dot_general | solution.py:60
  324.2 0.2 maximum_subtract_fusion
  324.4 1.3 copy.29
  325.7 3.6 %all-to-all-start.5 = ((f32[2,256,512]{1,0,2:T(2,128)}), f32[2,256,512]{1,0,2:T(2,128)S(1)}, u32[]{:S(2)}, u32[]{:S(2)}) async-start(f32[2,256,512]{1,0,2:T(2,128)} %copy.29), calls=%async_computation.5 | async-start | bytes 2097152 | tf_op jit(solution)/shard_map/all_to_all | solution.py:95
  330.5 15.5 %all-to-all-done.5 = f32[2,256,512]{1,0,2:T(2,128)S(1)} async-done(((f32[2,256,512]{1,0,2:T(2,128)}), f32[2,256,512]{1,0,2:T(2,128)S(1)}, u32[]{:S(2)}, u32[]{:S(2)}) %all-to-all-start.5) | async-done | bytes 1048608 | tf_op jit(solution)/shard_map/all_to_all | solution.py:95
  346.0 0.1 copy.30
  346.1 0.1 copy.33
  346.2 1.6 fusion.8
  (16 shorter events, 0.1 us)
Async XLA Ops:
  6.5 148.0 %copy-start = (f32[2048]{0:T(1024)S(1)}, f32[2048]{0:T(1024)}, u32[]{:S(2)}) copy-start(f32[2048]{0:T(1024)} %param.9) | copy-start | bytes 24580
  12.1 15.4 %all-to-all-start.1 = ((f32[8,2,128,64]{2,3,1,0:T(8,128)}), f32[8,2,128,64]{2,3,1,0:T(8,128)S(1)}, u32[]{:S(2)}, u32[]{:S(2)}) async-start(f32[8,2,128,64]{2,3,1,0:T(8,128)} %copy.21), calls=%async_computation.1 | async-start | bytes 1048576 | tf_op jit(solution)/shard_map/all_to_all | solution.py:33
  27.5 12.4 %all-to-all-start = ((f32[8,2,128,64]{2,3,1,0:T(8,128)}), f32[8,2,128,64]{2,3,1,0:T(8,128)S(1)}, u32[]{:S(2)}, u32[]{:S(2)}) async-start(f32[8,2,128,64]{2,3,1,0:T(8,128)} %copy.20), calls=%async_computation | async-start | bytes 1048576 | tf_op jit(solution)/shard_map/all_to_all | solution.py:33
  39.9 33.6 %all-to-all-start.3 = ((f32[8,2,128,256]{3,2,1,0:T(8,128)}), f32[8,2,128,256]{3,2,1,0:T(8,128)S(1)}, u32[]{:S(2)}, u32[]{:S(2)}) async-start(f32[8,2,128,256]{3,2,1,0:T(8,128)} %copy.25), calls=%async_computation.3 | async-start | bytes 4194304 | tf_op jit(solution)/shard_map/all_to_all | solution.py:33
  73.5 33.9 %all-to-all-start.2 = ((f32[8,2,128,256]{3,2,1,0:T(8,128)}), f32[8,2,128,256]{3,2,1,0:T(8,128)}, u32[]{:S(2)}, u32[]{:S(2)}) async-start(f32[8,2,128,256]{3,2,1,0:T(8,128)} %copy.24), calls=%async_computation.2 | async-start | bytes 4194304 | tf_op jit(solution)/shard_map/all_to_all | solution.py:33
  77.8 226.6 %all-reduce.2.cloned.1.call-start = ((), (), s32[]{:S(2)}) async-start(), calls=%async_computation.6 | async-start | bytes 16777216 | tf_op jit(solution)/shard_map/psum | solution.py:92
  81.0 29.7 %copy-start.3 = (f32[8,2,128,256]{2,3,0,1:T(8,128)S(1)}, f32[8,2,128,256]{2,3,0,1:T(8,128)}, u32[]{:S(2)}) copy-start(f32[8,2,128,256]{2,3,0,1:T(8,128)} %copy.27) | copy-start | bytes 6291460
  113.2 11.2 %copy-start.1 = (f32[1,256,8,256]{1,3,2,0:T(8,128)}, f32[1,256,8,256]{1,3,2,0:T(8,128)S(1)}, u32[]{:S(2)}) copy-start(f32[1,256,8,256]{1,3,2,0:T(8,128)S(1)} %get-tuple-element.7) | copy-start | bytes 6291460
  143.9 0.7 copy-start.6
  143.9 10.8 %copy-start.4 = (f32[8,2,256,64]{2,3,0,1:T(8,128)S(1)}, f32[8,2,256,64]{2,3,0,1:T(8,128)}, u32[]{:S(2)}) copy-start(f32[8,2,256,64]{2,3,0,1:T(8,128)} %get-tuple-element.13) | copy-start | bytes 3145732
  304.4 4.1 %copy-start.2 = (f32[1,256,8,256]{1,3,2,0:T(8,128)S(1)}, f32[1,256,8,256]{1,3,2,0:T(8,128)}, u32[]{:S(2)}) copy-start(f32[1,256,8,256]{1,3,2,0:T(8,128)} %copy-done.1) | copy-start | bytes 6291460
  320.3 3.9 %copy-start.5 = (f32[2,256,512]{2,1,0:T(8,128)S(1)}, f32[2,256,512]{2,1,0:T(8,128)}, u32[]{:S(2)}) copy-start(f32[2,256,512]{2,1,0:T(8,128)} %copy.28) | copy-start | bytes 3145732
  325.7 20.3 %all-to-all-start.5 = ((f32[2,256,512]{1,0,2:T(2,128)}), f32[2,256,512]{1,0,2:T(2,128)S(1)}, u32[]{:S(2)}, u32[]{:S(2)}) async-start(f32[2,256,512]{1,0,2:T(2,128)} %copy.29), calls=%async_computation.5 | async-start | bytes 2097152 | tf_op jit(solution)/shard_map/all_to_all | solution.py:95
Sparse Core Ops, SparseCore 0:
  144.1 160.2 all-reduce.1
where the time goes:
time: 359 us; the launch traced here: 355 us
  waiting for transfers between devices  229 us (64%)
  matrix products  42.2 us (12%)
  local copies, waits for them, and re-layouts  21.8 us (6%)
  starting transfers between devices  20.9 us (6%)
  between operations  16.2 us (5%)
  other arithmetic  15.9 us (4%)
  blocking collectives  8.52 us (2%)
    psum x1, waiting for transfers between devices, per_device(): margin = lax.psum(margin_of(row_waves, row_columns), ('ga', 'ba'))  148 us
    all_to_all x4, waiting for transfers between devices, cut_exchange(): lax.all_to_all(slab, axis, split_axis=0, concat_axis=0, tiled=True)  65.3 us
    dot_general x4, matrix products, tdot(): lax.dot_general(left, right, (((0,), (0,)), ((), ())), precision=lax.Prec...  26.5 us
    all_to_all x4, starting transfers between devices, cut_exchange(): lax.all_to_all(slab, axis, split_axis=0, concat_axis=0, tiled=True)  17.3 us
    dot_general x5, matrix products, mdot(): jnp.dot(left, right, precision=lax.Precision.HIGHEST, preferred_element_t...  15.8 us
    all_to_all x1, waiting for transfers between devices, per_device(): lax.all_to_all(row_result, 'ba', split_axis=2, concat_axis=1, tiled=True)  15.5 us
    split x6, local copies, waits for them, and re-layouts, cut_exchange(): jnp.split(blocks, edges_of(blocks.shape[split_at], pieces), axis=split_at)  10.5 us
    all_to_all x1, blocking collectives, from_everyone(): lax.all_to_all(jnp.broadcast_to(value[None], (count, *value.shape)), axis...  8.52 us
  transfers between devices with their start and end apart: 6, of which 6 were waited for; matrix products, arithmetic and copies ran while one was open for 4% of the time, Pallas kernels for 0%

commit v1 on v0

--- a/solution.py
+++ b/solution.py
@@ -89,7 +89,8 @@
     )
     all_panels = gather_directly(panel_band, "ba", 0)
     full_weight = weights_for(band_weight, all_panels)
-    margin = lax.psum(margin_of(row_waves, row_columns), ("ga", "ba"))
+    half = lax.psum(margin_of(row_waves, row_columns), "ga")
+    margin = lax.psum(half, "ba")
     weighted = margin * full_weight[None, :, None]
     row_result = row_columns - correct_with(row_waves, weighted)
     result = lax.all_to_all(row_result, "ba", split_axis=2, concat_axis=1, tiled=True)

time: 359 us -> 745 us (2.08)
  waiting for transfers between devices: 229 us -> 610 us
    psum x1 -> x2, waiting for transfers between devices: 148 us -> 530 us  [the longest x1 330 us: per_device(): margin = lax.psum(half, 'ba')]
  transfers between devices with their start and end apart: 6 -> 7, of which waited for: 6 -> 7; matrix products, arithmetic and copies ran while one was open for 4% -> 2% of each run, Pallas kernels for 0% -> 0%
where the time goes in v1:
time: 745 us; the launch traced here: 742 us
  waiting for transfers between devices  610 us (82%)
  matrix products  42.3 us (6%)
  starting transfers between devices  25.5 us (3%)
  local copies, waits for them, and re-layouts  21.8 us (3%)
  between operations  16.2 us (2%)
  other arithmetic  15.9 us (2%)
  blocking collectives  10.3 us (1%)
    psum x1, waiting for transfers between devices, per_device(): margin = lax.psum(half, 'ba')  330 us
    psum x1, waiting for transfers between devices, per_device(): half = lax.psum(margin_of(row_waves, row_columns), 'ga')  200 us
    all_to_all x4, waiting for transfers between devices, cut_exchange(): lax.all_to_all(slab, axis, split_axis=0, concat_axis=0, tiled=True)  65.3 us
    dot_general x4, matrix products, tdot(): lax.dot_general(left, right, (((0,), (0,)), ((), ())), precision=lax.Prec...  26.5 us
    all_to_all x4, starting transfers between devices, cut_exchange(): lax.all_to_all(slab, axis, split_axis=0, concat_axis=0, tiled=True)  17.3 us
    dot_general x5, matrix products, mdot(): jnp.dot(left, right, precision=lax.Precision.HIGHEST, preferred_element_t...  15.8 us
  transfers between devices with their start and end apart: 7, of which 7 were waited for; matrix products, arithmetic and copies ran while one was open for 2% of the time, Pallas kernels for 0%

profile of v1, /device:TPU:2, one launch (start us, length us, event | category | flops | bytes accessed | tf_op | source)
XLA Modules:
  0.0 741.5 jit_solution(5059571646338722396)
XLA Ops:
  6.5 1.2 dynamic_slice.6
  8.9 1.8 fusion.9
  10.8 0.3 copy.34
  11.2 0.9 copy.21
  12.1 5.8 all-to-all-start.1
  17.9 0.9 copy.20
  18.8 8.7 %all-to-all-done.1 = f32[8,2,128,64]{2,3,1,0:T(8,128)S(1)} async-done(((f32[8,2,128,64]{2,3,1,0:T(8,128)}), f32[8,2,128,64]{2,3,1,0:T(8,128)S(1)}, u32[]{:S(2)}, u32[]{:S(2)}) %all-to-all-start.1) | async-done | bytes 524320 | tf_op jit(solution)/shard_map/all_to_all | solution.py:33
  27.5 3.5 all-to-all-start
  31.0 4.0 fusion.13
  34.9 1.6 copy.25
  36.5 3.4 all-to-all-done
  39.9 3.6 all-to-all-start.3
  43.5 3.1 copy.24
  46.6 26.9 %all-to-all-done.3 = f32[8,2,128,256]{3,2,1,0:T(8,128)S(1)} async-done(((f32[8,2,128,256]{3,2,1,0:T(8,128)}), f32[8,2,128,256]{3,2,1,0:T(8,128)S(1)}, u32[]{:S(2)}, u32[]{:S(2)}) %all-to-all-start.3) | async-done | bytes 2097184 | tf_op jit(solution)/shard_map/all_to_all | solution.py:33
  73.5 4.3 all-to-all-start.2
  77.9 1.1 copy_bitcast_fusion
  79.0 0.1 fusion.14
  79.1 1.9 copy.27
  81.0 26.4 %all-to-all-done.2 = f32[8,2,128,256]{3,2,1,0:T(8,128)} async-done(((f32[8,2,128,256]{3,2,1,0:T(8,128)}), f32[8,2,128,256]{3,2,1,0:T(8,128)}, u32[]{:S(2)}, u32[]{:S(2)}) %all-to-all-start.2) | async-done | bytes 2097184 | tf_op jit(solution)/shard_map/all_to_all | solution.py:33
  107.4 3.3 copy.26
  110.7 2.1 maximum_bitcast_fusion
  112.8 0.4 fusion.12
  113.2 3.7 fusion.17
  116.9 3.7 fusion.16
  120.7 3.8 subtract_bitcast_fusion
  124.4 15.3 %add_bitcast_fusion = f32[1,2048,512]{2,1,0:T(8,128)S(1)} fusion(f32[2048,512]{1,0:T(8,128)S(1)} %fusion.16, f32[256,2048]{0,1:T(8,128)S(1)} %bitcast.73, f32[256,512]{0,1:T(8,128)S(1)} %bitcast.77), kind=kOutput, calls=%fused_computation.6 | convolution fusion | flops 3222274048 | bytes 11010048 | tf_op jit(solution)/shard_map/dot_general | solution.py:50
  139.8 4.2 pad_maximum_fusion
  144.1 199.6 %all-reduce.3.cloned.1.call-done = f32[2,2048,512]{2,1,0:T(8,128)} async-done(((f32[2,2048,512]{2,1,0:T(8,128)}), f32[2,2048,512]{2,1,0:T(8,128)}) %all-reduce.3.cloned.1.call-update) | async-done | bytes 8388624 | tf_op jit(solution)/shard_map/psum | solution.py:92
  343.7 0.6 copy-done.6
  344.3 10.3 %all_to_all.44 = s32[8,1,2]{2,1,0:T(1,128)S(1)} all-to-all(s32[8,1,2]{2,1,0:T(1,128)S(1)} %broadcast_in_dim.2), channel_id=1, replica_groups=mesh['ga'=16,'ba'=8] {'ba'}, dimensions={0} | all-to-all | bytes 128 | tf_op jit(solution)/shard_map/all_to_all | solution.py:39
  354.6 0.6 broadcast.7
  355.2 0.7 reduce.3
  355.9 0.1 eq.17
  356.0 0.2 convolution_bitcast_fusion
  356.2 1.3 copy.28
  357.5 330.0 %all-reduce.5.cloned.1.call-done = f32[2,2048,512]{2,1,0:T(8,128)} async-done(((f32[2,2048,512]{2,1,0:T(8,128)}), f32[2,2048,512]{2,1,0:T(8,128)}) %all-reduce.5.cloned.1.call-update) | async-done | bytes 8388624 | tf_op jit(solution)/shard_map/psum | solution.py:93
  687.5 4.1 broadcast_multiply_fusion
  691.7 3.8 fusion
  695.5 3.9 fusion.1
  699.4 4.1 fusion.7
  703.4 3.8 fusion.5
  707.3 0.2 maximum_subtract_fusion
  707.5 1.3 copy.29
  708.8 8.1 %all-to-all-start.5 = ((f32[2,256,512]{1,0,2:T(2,128)}), f32[2,256,512]{1,0,2:T(2,128)S(1)}, u32[]{:S(2)}, u32[]{:S(2)}) async-start(f32[2,256,512]{1,0,2:T(2,128)} %copy.29), calls=%async_computation.5 | async-start | bytes 2097152 | tf_op jit(solution)/shard_map/all_to_all | solution.py:96
  718.1 14.6 %all-to-all-done.5 = f32[2,256,512]{1,0,2:T(2,128)S(1)} async-done(((f32[2,256,512]{1,0,2:T(2,128)}), f32[2,256,512]{1,0,2:T(2,128)S(1)}, u32[]{:S(2)}, u32[]{:S(2)}) %all-to-all-start.5) | async-done | bytes 1048608 | tf_op jit(solution)/shard_map/all_to_all | solution.py:96
  732.7 0.1 copy.30
  732.8 0.1 copy.33
  732.9 1.6 fusion.8
  (19 shorter events, 0.2 us)
Async XLA Ops:
  6.5 349.4 %copy-start = (f32[2048]{0:T(1024)S(1)}, f32[2048]{0:T(1024)}, u32[]{:S(2)}) copy-start(f32[2048]{0:T(1024)} %param.9) | copy-start | bytes 24580
  12.1 15.4 %all-to-all-start.1 = ((f32[8,2,128,64]{2,3,1,0:T(8,128)}), f32[8,2,128,64]{2,3,1,0:T(8,128)S(1)}, u32[]{:S(2)}, u32[]{:S(2)}) async-start(f32[8,2,128,64]{2,3,1,0:T(8,128)} %copy.21), calls=%async_computation.1 | async-start | bytes 1048576 | tf_op jit(solution)/shard_map/all_to_all | solution.py:33
  27.5 12.4 %all-to-all-start = ((f32[8,2,128,64]{2,3,1,0:T(8,128)}), f32[8,2,128,64]{2,3,1,0:T(8,128)S(1)}, u32[]{:S(2)}, u32[]{:S(2)}) async-start(f32[8,2,128,64]{2,3,1,0:T(8,128)} %copy.20), calls=%async_computation | async-start | bytes 1048576 | tf_op jit(solution)/shard_map/all_to_all | solution.py:33
  39.9 33.6 %all-to-all-start.3 = ((f32[8,2,128,256]{3,2,1,0:T(8,128)}), f32[8,2,128,256]{3,2,1,0:T(8,128)S(1)}, u32[]{:S(2)}, u32[]{:S(2)}) async-start(f32[8,2,128,256]{3,2,1,0:T(8,128)} %copy.25), calls=%async_computation.3 | async-start | bytes 4194304 | tf_op jit(solution)/shard_map/all_to_all | solution.py:33
  73.5 33.9 %all-to-all-start.2 = ((f32[8,2,128,256]{3,2,1,0:T(8,128)}), f32[8,2,128,256]{3,2,1,0:T(8,128)}, u32[]{:S(2)}, u32[]{:S(2)}) async-start(f32[8,2,128,256]{3,2,1,0:T(8,128)} %copy.24), calls=%async_computation.2 | async-start | bytes 4194304 | tf_op jit(solution)/shard_map/all_to_all | solution.py:33
  77.8 265.9 %all-reduce.3.cloned.1.call-start = ((), (), s32[]{:S(2)}) async-start(), calls=%async_computation.6 | async-start | bytes 16777216 | tf_op jit(solution)/shard_map/psum | solution.py:92
  81.0 29.7 %copy-start.3 = (f32[8,2,128,256]{2,3,0,1:T(8,128)S(1)}, f32[8,2,128,256]{2,3,0,1:T(8,128)}, u32[]{:S(2)}) copy-start(f32[8,2,128,256]{2,3,0,1:T(8,128)} %copy.27) | copy-start | bytes 6291460
  113.2 11.2 %copy-start.1 = (f32[1,256,8,256]{1,3,2,0:T(8,128)}, f32[1,256,8,256]{1,3,2,0:T(8,128)S(1)}, u32[]{:S(2)}) copy-start(f32[1,256,8,256]{1,3,2,0:T(8,128)S(1)} %get-tuple-element.7) | copy-start | bytes 6291460
  144.0 543.5 %all-reduce.5.cloned.1.call-start = ((), (), s32[]{:S(2)}) async-start(), calls=%async_computation.7 | async-start | bytes 16777216 | tf_op jit(solution)/shard_map/psum | solution.py:93
  343.7 0.7 copy-start.6
  343.7 12.5 %copy-start.4 = (f32[8,2,256,64]{2,3,0,1:T(8,128)S(1)}, f32[8,2,256,64]{2,3,0,1:T(8,128)}, u32[]{:S(2)}) copy-start(f32[8,2,256,64]{2,3,0,1:T(8,128)} %get-tuple-element.13) | copy-start | bytes 3145732
  687.5 4.1 copy-start.2
  703.4 3.9 copy-start.5
  708.8 23.9 %all-to-all-start.5 = ((f32[2,256,512]{1,0,2:T(2,128)}), f32[2,256,512]{1,0,2:T(2,128)S(1)}, u32[]{:S(2)}, u32[]{:S(2)}) async-start(f32[2,256,512]{1,0,2:T(2,128)} %copy.29), calls=%async_computation.5 | async-start | bytes 2097152 | tf_op jit(solution)/shard_map/all_to_all | solution.py:96
Sparse Core Ops, SparseCore 0:
  144.1 199.5 all-reduce.2
  346.2 341.2 all-reduce.4
